TPU v7x, 32 devices: a whole 2x2x4 slice. The times are simulated.
32 devices in a mesh: parts: 2 (over x), dp: 16 (over z, y, core).
Axes of the slice: x: 2, y: 2, z: 4, core: 2. Of those that a mesh axis runs over, the one named last changes fastest.
Arguments:
- activations: bfloat16 [8192, 14336], P(('parts', 'dp')), parts along dimension 0, may hold values from -6 to 6
- out_grads: bfloat16 [8192, 4096], P(('parts', 'dp')), parts along dimension 0, may hold values from -6 to 6
- lengths: int32 [32, 4], P(('parts', 'dp')), parts along dimension 0, may hold values from 1 to 128, 256 in all within a row
- proj_in: bfloat16 [14336, 64], replicated, may hold values from -0.046875 to 0.046875
- proj_out: bfloat16 [4096, 64], replicated, may hold values from -0.09375 to 0.09375
- queries: bfloat16 [1024, 4096], P(('parts', 'dp')), parts along dimension 0, may hold values from -0.01171875 to 0.01171875
Outputs:
- scores: bfloat16 [128, 512], P(('parts', 'dp')), parts along dimension 0
There are 2 independent parts, one for each index of `parts`. A program takes and returns all parts, laid end to end along the dimension named above; an argument that names none is the same for every part. Nothing has to cross between parts.
Inputs may be any that keep to these rules, and one draw needn't show every extreme that they name: Each row of lengths sums to 256, and one entry of each row equals 128.
All inputs are finite; a program needn't handle non-finite values.
Results may differ from a plain program's by a relative error of at most 0.0065.
Values may be sent and summed in bfloat16 or wider, within the bound.
A program may use at most 128 MiB of HBM per device.

v0:
```python
import functools

import jax
import jax.numpy as jnp
from jax import lax
from jax.experimental import pallas as pl
from jax.experimental.pallas import tpu as pltpu
from jax.sharding import PartitionSpec as P

MESH = pl.DeviceIdType.MESH
NT = (((1,), (1,)), ((), ()))
NN = (((1,), (0,)), ((), ()))
CHUNKS = (4, 4, 4, 4)
PIECES = 4
GROUP = 4


def kernel(
    n,
    lens_hbm,
    acts_hbm,
    grads_hbm,
    win_hbm,
    wout_hbm,
    q_hbm,
    out_hbm,
    lens,
    acts,
    grads,
    win,
    wout,
    qs,
    expand,
    acc,
    stage,
    result,
    out_vmem,
    local_sem,
    acts_sem,
    grads_sem,
    win_sem,
    q_send,
    q_recv,
    row_send,
    row_recv,
    mask_send,
    mask_recv,
    res_send,
    res_recv,
    *per_chunk,
):
    count = len(per_chunk) // 2
    rows, masks = per_chunk[:count], per_chunk[count:]
    me = lax.axis_index("dp")
    n_groups = n // GROUP
    group, lane = me // GROUP, lax.rem(me, GROUP)
    n_half, per_half, _, width = rows[0].shape
    sizes = [ref.shape[2] for ref in rows]
    starts = [sum(sizes[:c]) for c in range(count)]
    ex = stage.shape[1]
    rank = width // 2
    pairs = rank // 2
    half, slot = group // per_half, lax.rem(group, per_half)
    ff = acts.shape[1]
    piece = ff // PIECES

    backward = (group < n_groups - group).astype(jnp.int32)

    def turn(t):
        return t + backward * (n_groups - 2 * t)

    def peer(t):
        t = turn(t)
        return lax.rem(group + t, n_groups) * GROUP + lane

    buddy = me + 1 - 2 * lax.rem(me, 2)
    across = me + 2 - 4 * lax.rem(me // 2, 2)
    across_lane = lax.rem(across, GROUP)

    def start(source, target, sem):
        load = pltpu.make_async_copy(source, target, sem)
        load.start()
        return load

    pieces = [pl.ds(p * piece, piece) for p in range(PIECES)]
    spans = [pl.ds(starts[c], sizes[c]) for c in range(count)]
    load_grads, load_acts = {}, {}

    def fetch_grads(c):
        span = spans[c]
        load_grads[c] = start(grads_hbm.at[span], grads.at[span], grads_sem.at[c])

    def fetch_acts(c, p):
        part = (spans[c], pieces[p])
        load_acts[c, p] = start(acts_hbm.at[*part], acts.at[*part], acts_sem.at[c, p])

    def fetch(c):
        if c < count:
            fetch_grads(c)
            for p in range(PIECES):
                fetch_acts(c, p)

    load_win = []
    for p in range(PIECES):
        part = win.at[:, pieces[p]]
        load_win.append(start(win_hbm.at[:, pieces[p]], part, win_sem.at[p]))
        fetch_acts(0, p)
    load_wout = start(wout_hbm, wout, local_sem.at[1])
    fetch_grads(0)
    load_lens = start(lens_hbm, lens, local_sem.at[3])
    load_q = start(q_hbm, qs.at[lane], local_sem.at[0])
    fetch(1)

    barrier = pltpu.get_barrier_semaphore()
    peers = [peer(t) for t in range(1, n_groups)]
    for other in peers + [buddy, across]:
        pl.semaphore_signal(barrier, inc=1, device_id={"dp": other}, device_id_type=MESH)

    row_copies = []
    for c in range(count):
        span = spans[c]
        total = jnp.zeros((rank, sizes[c]), jnp.float32)
        for p in range(PIECES):
            if c == 0:
                load_win[p].wait()
            load_acts[c, p].wait()
            if p == 0:
                fetch(c + 2)
            total = total + lax.dot_general(
                win[:, pieces[p]], acts[span, pieces[p]], NT, preferred_element_type=jnp.float32
            )
        if c == 0:
            load_wout.wait()
        load_grads[c].wait()
        other = lax.dot_general(wout[...], grads[span], NT, preferred_element_type=jnp.float32)
        both = jnp.concatenate([other, total], axis=0)
        rows[c][half, slot] = both.T.astype(jnp.bfloat16)
        if c == 0:
            load_lens.wait()
            for k in range(count):
                shape = masks[k].shape[1:]
                row_id = lax.broadcasted_iota(jnp.int32, shape, 0) - slot * ex
                lane_id = lax.broadcasted_iota(jnp.int32, shape, 1) - slot * sizes[k]
                inside = (lane_id >= 0) & (lane_id < sizes[k])
                token = lane_id + starts[k]
                first = jnp.int32(0)
                mask = jnp.zeros(shape, jnp.float32)
                for e in range(ex):
                    end = first + lens[0, e]
                    hit = inside & (row_id == e) & (token >= first) & (token < end)
                    mask = jnp.where(hit, 1.0, mask)
                    first = end
                masks[k][group] = mask
            r_id = lax.broadcasted_iota(jnp.int32, (16 * pairs, width), 0)
            c_id = lax.broadcasted_iota(jnp.int32, (16 * pairs, width), 1)
            odd = (r_id >= 8 * pairs).astype(jnp.int32)
            source = 2 * ((r_id - odd * 8 * pairs) // 8) + odd
            expand[...] = jnp.where(source == c_id, 1.0, 0.0).astype(jnp.bfloat16)
            acc[...] = jnp.zeros_like(acc)
            pl.semaphore_wait(barrier, len(peers) + 2)

            load_q.wait()
            q_copies = []
            for i, other in enumerate((across, buddy)):
                copy = pltpu.make_async_remote_copy(
                    src_ref=qs.at[lane],
                    dst_ref=qs.at[lane],
                    send_sem=q_send.at[i],
                    recv_sem=q_recv.at[i],
                    device_id={"dp": other},
                    device_id_type=MESH,
                )
                copy.start()
                q_copies.append(copy)
            mask_copies = []
            for k, t in [(k, t) for k in range(count) for t in range(1, n_groups)]:
                copy = pltpu.make_async_remote_copy(
                    src_ref=masks[k].at[group],
                    dst_ref=masks[k].at[group],
                    send_sem=mask_send.at[turn(t) - 1, k],
                    recv_sem=mask_recv.at[turn(t) - 1, k],
                    device_id={"dp": peer(t)},
                    device_id_type=MESH,
                )
                copy.start()
                mask_copies.append(copy)
        copies = []
        for t in range(1, n_groups):
            copy = pltpu.make_async_remote_copy(
                src_ref=rows[c].at[half, slot],
                dst_ref=rows[c].at[half, slot],
                send_sem=row_send.at[turn(t) - 1, c],
                recv_sem=row_recv.at[turn(t) - 1, c],
                device_id={"dp": peer(t)},
                device_id_type=MESH,
            )
            copy.start()
            copies.append(copy)
        row_copies.append(copies)

    def gather(c):
        for copy in row_copies[c]:
            copy.wait_recv()
        for h in range(n_half):
            block = rows[c][h].reshape(per_half * sizes[c], width)
            mask = masks[c][h * per_half]
            for s in range(1, per_half):
                mask = mask + masks[c][h * per_half + s]
            wide = lax.dot_general(expand[...], block, NT, preferred_element_type=jnp.float32)
            wide = wide.reshape(2 * pairs, 8, mask.shape[1]) * mask[None]
            wide = wide.reshape(16 * pairs, mask.shape[1]).astype(jnp.bfloat16)
            acc[h] += lax.dot_general(wide, block, NN, preferred_element_type=jnp.float32)

    for copy in mask_copies:
        copy.wait_recv()
    for c in range(count - 2):
        gather(c)
    q_copies[0].wait_recv()
    relay = pltpu.make_async_remote_copy(
        src_ref=qs.at[across_lane],
        dst_ref=qs.at[across_lane],
        send_sem=q_send.at[2],
        recv_sem=q_recv.at[2],
        device_id={"dp": buddy},
        device_id_type=MESH,
    )
    relay.start()
    for c in range(count - 2, count):
        gather(c)

    lower = lax.broadcasted_iota(jnp.int32, (8, width), 1) < rank
    columns = []
    for k in range(pairs):
        parts = []
        for h in range(n_half):
            even = pltpu.roll(acc[h, 8 * k : 8 * k + 8], rank, 1)
            odd_rows = acc[h, 8 * pairs + 8 * k : 8 * pairs + 8 * k + 8]
            parts.append(jnp.where(lower, even, odd_rows))
        columns.append(jnp.concatenate(parts, axis=0).astype(jnp.bfloat16))
    example_grads = jnp.concatenate(columns, axis=1)
    q_copies[1].wait_recv()
    relay.wait_recv()
    queries = qs[...].reshape(qs.shape[0] * qs.shape[1], qs.shape[2])
    scores = lax.dot_general(example_grads, queries, NT, preferred_element_type=jnp.float32)
    for s in range(n_groups):
        stage[s] = scores[s * ex : (s + 1) * ex].astype(jnp.bfloat16)
    res_copies = []
    for t in range(1, n_groups):
        copy = pltpu.make_async_remote_copy(
            src_ref=stage.at[lax.rem(group + turn(t), n_groups)],
            dst_ref=result.at[group],
            send_sem=res_send.at[turn(t) - 1],
            recv_sem=res_recv.at[turn(t) - 1],
            device_id={"dp": peer(t)},
            device_id_type=MESH,
        )
        copy.start()
        res_copies.append(copy)
    result[group] = stage[group]
    for copy in res_copies:
        copy.wait_recv()
    cols = qs.shape[0] * qs.shape[1]
    for s in range(n_groups):
        out_vmem[:, s * cols : (s + 1) * cols] = result[s]
    store = pltpu.make_async_copy(out_vmem, out_hbm, local_sem.at[4])
    store.start()
    for copy in q_copies + [relay] + mask_copies + res_copies:
        copy.wait_send()
    for copies in row_copies:
        for copy in copies:
            copy.wait_send()
    store.wait()


def local(n, activations, out_grads, lengths, proj_in, proj_out, queries):
    tokens, ff = activations.shape
    d = out_grads.shape[1]
    rank = proj_in.shape[1]
    ex = lengths.shape[1]
    nq, params = queries.shape
    n_groups = n // GROUP
    per_half = 8 // ex
    n_half = n_groups // per_half
    sizes = [tokens * part // sum(CHUNKS) for part in CHUNKS]
    count = len(sizes)
    width = 2 * rank
    bf16, f32 = jnp.bfloat16, jnp.float32
    dma = pltpu.SemaphoreType.DMA
    others = n_groups - 1
    hbm = pl.BlockSpec(memory_space=pltpu.MemorySpace.HBM)
    return pl.pallas_call(
        functools.partial(kernel, n),
        out_shape=jax.ShapeDtypeStruct((ex, nq * n), bf16),
        in_specs=[hbm] * 6,
        out_specs=pl.BlockSpec(memory_space=pl.ANY),
        scratch_shapes=[
            pltpu.SMEM((1, ex), jnp.int32),
            pltpu.VMEM((tokens, ff), bf16),
            pltpu.VMEM((tokens, d), bf16),
            pltpu.VMEM((rank, ff), bf16),
            pltpu.VMEM((rank, d), bf16),
            pltpu.VMEM((GROUP, nq, params), bf16),
            pltpu.VMEM((8 * rank, width), bf16),
            pltpu.VMEM((n_half, 8 * rank, width), f32),
            pltpu.VMEM((n_groups, ex, GROUP * nq), bf16),
            pltpu.VMEM((n_groups, ex, GROUP * nq), bf16),
            pltpu.VMEM((ex, nq * n), bf16),
            dma((5,)),
            dma((count, PIECES)),
            dma((count,)),
            dma((PIECES,)),
            dma((3,)),
            dma((3,)),
            dma((others, count)),
            dma((others, count)),
            dma((others, count)),
            dma((others, count)),
            dma((others,)),
            dma((others,)),
        ]
        + [pltpu.VMEM((n_half, per_half, size, width), bf16) for size in sizes]
        + [pltpu.VMEM((n_groups, 8, per_half * size), f32) for size in sizes],
        compiler_params=pltpu.CompilerParams(
            collective_id=0, has_side_effects=True, vmem_limit_bytes=56500000
        ),
    )(pltpu.with_memory_space_constraint(lengths, pltpu.HBM), activations, out_grads, proj_in.T, proj_out.T, queries)


def solution(mesh):
    in_specs = (
        P(("parts", "dp"), None),
        P(("parts", "dp"), None),
        P(("parts", "dp"), None),
        P(),
        P(),
        P(("parts", "dp"), None),
    )
    out_specs = P(("parts", "dp"), None)
    body = functools.partial(local, mesh.shape["dp"])
    return jax.shard_map(body, mesh=mesh, in_specs=in_specs, out_specs=out_specs, check_vma=False)
```

profile of v0, /device:TPU:0, one launch (start us, length us, event | category | flops | bytes accessed | tf_op | source)
XLA Modules:
  0.0 20.9 jit_solution(3430568902191630443)
XLA Ops:
  0.0 20.3 %shard_map.64 = bf16[4,512]{1,0:T(4,128)(2,1)S(1)} custom-call(s32[1,4]{1,0:T(1,128)} %lens_hbm.1, bf16[256,14336]{1,0:T(8,128)(2,1)} %acts_hbm.1, bf16[256,4096]{1,0:T(8,128)(2,1)} %grads_hbm.1, bf16[64,14336]{1,0:T(8,128)(2,1)} %bitcast.2, bf16[64,4096]{1,0:T(8,128)(2,1)} %bitcast.3, bf16[32,4096]{1,0:T(8,128)(2,1)} %q_hbm.1), custom_call_target="tpu_custom_call" | custom-call | tf_op jit(solution)/shard_map/pallas_call | solution.py:291
  20.3 0.6 %copy.8 = bf16[4,512]{1,0:T(4,128)(2,1)} copy(bf16[4,512]{1,0:T(4,128)(2,1)S(1)} %shard_map.64) | data formatting | bytes 8192
where the time goes:
time: 21 us; the launch traced here: 20.9 us
  Pallas kernels  20.3 us (97%)
  local copies, waits for them, and re-layouts  0.6 us (3%)
    pallas_call x1, Pallas kernels, local(): pl.pallas_call(functools.partial(kernel, n), out_shape=jax.ShapeDtypeStru...  20.3 us
    unnamed x1, local copies, waits for them, and re-layouts  0.6 us

commit v1 on v0

v1 whole, which is shorter than its diff:
```python
import functools

import jax
import jax.numpy as jnp
from jax import lax
from jax.experimental import pallas as pl
from jax.experimental.pallas import tpu as pltpu
from jax.sharding import PartitionSpec as P

MESH = pl.DeviceIdType.MESH
NT = (((1,), (1,)), ((), ()))
NN = (((1,), (0,)), ((), ()))
PIECES = 8
EARLY = 1
AHEAD = 4
GROUP = 4
LANES = 128
ROWS = 16


def kernel(
    n,
    lens_hbm,
    acts_hbm,
    grads_hbm,
    win_hbm,
    wout_hbm,
    q_hbm,
    out,
    lens,
    acts,
    grads,
    win,
    wout,
    qs,
    eg,
    stage,
    local_sem,
    piece_sem,
    send_sem,
    buddy_recv,
    across_recv,
    relay_recv,
    eg_recv,
    res_recv,
):
    me = lax.axis_index("dp")
    n_groups = n // GROUP
    group, lane = me // GROUP, lax.rem(me, GROUP)
    tokens, ff = acts.shape
    rank = win.shape[0]
    ex = stage.shape[1]
    slots = ROWS // ex
    nq, params = qs.shape[1:]
    span = params // slots
    tiles = span // LANES
    half = tiles * ROWS
    cols = GROUP * nq
    piece = ff // PIECES

    backward = (group < n_groups - group).astype(jnp.int32)

    def project(rows, weights, at, size):
        parts = []
        for h in range(2):
            first = at + h * (size // 2 // LANES * LANES)
            last = at + (size // 2 // LANES * LANES if h == 0 else size)
            one = weights[:, first:last]
            twice = jnp.concatenate([one, one], axis=0)
            parts.append(
                lax.dot_general(rows[:, first:last], twice, NT, preferred_element_type=jnp.float32)
            )
        return parts[0] + parts[1]

    def turn(t):
        return t + backward * (n_groups - 2 * t)

    def peer(t):
        return lax.rem(group + turn(t), n_groups) * GROUP + lane

    buddy = me + 1 - 2 * lax.rem(me, 2)
    across = me + 2 - 4 * lax.rem(me // 2, 2)
    across_lane = lax.rem(across, GROUP)

    def start(source, target, sem):
        load = pltpu.make_async_copy(source, target, sem)
        load.start()
        return load

    load_q = start(q_hbm, qs.at[lane], local_sem.at[0])
    load_lens = start(lens_hbm, lens, local_sem.at[1])
    load_wout = start(wout_hbm, wout, local_sem.at[2])
    load_grads = start(grads_hbm, grads, local_sem.at[2])
    pieces = [pl.ds(p * piece, piece) for p in range(PIECES)]
    loads = {}

    def fetch(p):
        if p < PIECES:
            loads[p] = (
                start(win_hbm.at[:, pieces[p]], win.at[:, pieces[p]], piece_sem.at[p]),
                start(acts_hbm.at[:, pieces[p]], acts.at[:, pieces[p]], piece_sem.at[p]),
            )

    for p in range(EARLY):
        fetch(p)

    barrier = pltpu.get_barrier_semaphore()
    peers = [peer(t) for t in range(1, n_groups)]
    for other in peers + [buddy, across]:
        pl.semaphore_signal(barrier, inc=1, device_id={"dp": other}, device_id_type=MESH)

    def send(source, target, recv_sem, other):
        copy = pltpu.make_async_remote_copy(
            src_ref=source,
            dst_ref=target,
            send_sem=send_sem,
            recv_sem=recv_sem,
            device_id={"dp": other},
            device_id_type=MESH,
        )
        copy.start()
        return copy

    load_q.wait()
    for p in range(EARLY, AHEAD):
        fetch(p)
    pl.semaphore_wait(barrier, len(peers) + 2)
    sent = []
    across_copies = []
    for s in range(slots):
        part = qs.at[lane, :, pl.ds(s * span, span)]
        across_copies.append(send(part, part, across_recv.at[s], across))
    buddy_copy = send(qs.at[lane], qs.at[lane], buddy_recv, buddy)
    sent += across_copies + [buddy_copy]

    load_lens.wait()
    token = lax.broadcasted_iota(jnp.int32, (8, tokens), 1)
    row_ex = lax.rem(lax.broadcasted_iota(jnp.int32, (8, tokens), 0), ex)
    first = jnp.int32(0)
    mask = jnp.zeros((8, tokens), jnp.float32)
    for e in range(ex):
        end = first + lens[0, e]
        mask = jnp.where((row_ex == e) & (token >= first) & (token < end), 1.0, mask)
        first = end

    r_id = lax.broadcasted_iota(jnp.int32, (2 * half, 2 * rank), 0)
    c_id = lax.broadcasted_iota(jnp.int32, (2 * half, 2 * rank), 1)
    odd = (r_id >= half).astype(jnp.int32)
    inner = r_id - odd * half
    source = 2 * (lax.rem(inner // ex, slots) * tiles + inner // ROWS) + odd
    expand = jnp.where(source == c_id, 1.0, 0.0).astype(jnp.bfloat16)

    load_wout.wait()
    load_grads.wait()
    proj_grads = project(grads, wout, 0, wout.shape[1]).astype(jnp.bfloat16)
    wide = lax.dot_general(expand, proj_grads, NT, preferred_element_type=jnp.float32)
    wide = wide.reshape(2 * half // 8, 8, tokens) * mask[None]
    wide = wide.reshape(2 * half, tokens).astype(jnp.bfloat16)

    total = jnp.zeros((tokens, 2 * rank), jnp.float32)
    for p in range(PIECES):
        for load in loads[p]:
            load.wait()
        fetch(p + AHEAD)
        total = total + project(acts, win, p * piece, piece)
    proj_acts = total.astype(jnp.bfloat16)
    outer = lax.dot_general(wide, proj_acts, NN, preferred_element_type=jnp.float32)
    lower = lax.broadcasted_iota(jnp.int32, (half, 2 * rank), 1) < rank
    eg[group] = jnp.where(lower, outer[:half], outer[half:]).astype(jnp.bfloat16)

    eg_copies = []
    for t in range(1, n_groups):
        eg_copies.append(send(eg.at[group], eg.at[group], eg_recv, peer(t)))

    relays = []
    for s in range(slots):
        across_copies[s].wait_recv()
        part = qs.at[across_lane, :, pl.ds(s * span, span)]
        relays.append(send(part, part, relay_recv.at[s], buddy))
    buddy_copy.wait_recv()
    others = pl.ds(0, n_groups - 1)
    pltpu.make_async_copy(eg.at[others], eg.at[others], eg_recv).wait()

    stacked = []
    for g in range(n_groups):
        one = eg[g]
        stacked.append(
            jnp.concatenate([one[ROWS * t : ROWS * (t + 1)] for t in range(tiles)], axis=1)
        )
    stacked = jnp.concatenate(stacked, axis=0)
    scores = [jnp.zeros((ex, cols), jnp.float32) for _ in range(n_groups)]
    for s in range(slots):
        relays[s].wait_recv()
        queries = qs[:, :, pl.ds(s * span, span)].reshape(cols, span)
        term = 0.0
        for h in range(2):
            side = slice(h * (span // 2), (h + 1) * (span // 2))
            term = term + lax.dot_general(
                stacked[:, side], queries[:, side], NT, preferred_element_type=jnp.float32
            )
        for g in range(n_groups):
            row = ROWS * g + ex * s
            scores[g] = scores[g] + term[row : row + ex]
    for g in range(n_groups):
        stage[g] = scores[g].astype(jnp.bfloat16)

    own = pl.ds(pl.multiple_of(group * cols, LANES), cols)
    res_copies = []
    for t in range(1, n_groups):
        target = lax.rem(group + turn(t), n_groups)
        res_copies.append(
            send(stage.at[target], out.at[:, own], res_recv, peer(t))
        )
    out[:, own] = stage[group]
    rest = out.at[:, pl.ds(0, (n_groups - 1) * cols)]
    pltpu.make_async_copy(rest, rest, res_recv).wait()
    for copy in sent + eg_copies + relays + res_copies:
        copy.wait_send()


def local(n, activations, out_grads, lengths, proj_in, proj_out, queries):
    tokens, ff = activations.shape
    d = out_grads.shape[1]
    rank = proj_in.shape[1]
    ex = lengths.shape[1]
    nq, params = queries.shape
    n_groups = n // GROUP
    slots = ROWS // ex
    bf16 = jnp.bfloat16
    dma = pltpu.SemaphoreType.DMA
    hbm = pl.BlockSpec(memory_space=pltpu.MemorySpace.HBM)
    return pl.pallas_call(
        functools.partial(kernel, n),
        out_shape=jax.ShapeDtypeStruct((ex, nq * n), bf16),
        in_specs=[hbm] * 6,
        out_specs=pl.BlockSpec(memory_space=pltpu.MemorySpace.VMEM),
        scratch_shapes=[
            pltpu.SMEM((1, ex), jnp.int32),
            pltpu.VMEM((tokens, ff), bf16),
            pltpu.VMEM((tokens, d), bf16),
            pltpu.VMEM((rank, ff), bf16),
            pltpu.VMEM((rank, d), bf16),
            pltpu.VMEM((GROUP, nq, params), bf16),
            pltpu.VMEM((n_groups, ex * params // LANES, LANES), bf16),
            pltpu.VMEM((n_groups, ex, GROUP * nq), bf16),
            dma((3,)),
            dma((PIECES,)),
            dma,
            dma,
            dma((slots,)),
            dma((slots,)),
            dma,
            dma,
        ],
        compiler_params=pltpu.CompilerParams(
            collective_id=0, has_side_effects=True, vmem_limit_bytes=56500000
        ),
    )(pltpu.with_memory_space_constraint(lengths, pltpu.HBM), activations, out_grads, proj_in.T, proj_out.T, queries)


def solution(mesh):
    in_specs = (
        P(("parts", "dp"), None),
        P(("parts", "dp"), None),
        P(("parts", "dp"), None),
        P(),
        P(),
        P(("parts", "dp"), None),
    )
    out_specs = P(("parts", "dp"), None)
    body = functools.partial(local, mesh.shape["dp"])
    return jax.shard_map(body, mesh=mesh, in_specs=in_specs, out_specs=out_specs, check_vma=False)
```

time: 21 us -> 19.7 us (0.938)
  Pallas kernels: 20.3 us -> 18.9 us
    pallas_call x1, Pallas kernels: 20.3 us -> 18.9 us  [local(): pl.pallas_call(functools.partial(kernel, n), out_shape=jax.ShapeDtypeStru...]
where the time goes in v1:
time: 19.7 us; the launch traced here: 19.5 us
  Pallas kernels  18.9 us (96%)
  local copies, waits for them, and re-layouts  0.6 us (3%)
    pallas_call x1, Pallas kernels, local(): pl.pallas_call(functools.partial(kernel, n), out_shape=jax.ShapeDtypeStru...  18.9 us
    unnamed x1, local copies, waits for them, and re-layouts  0.6 us

profile of v1, /device:TPU:0, one launch (start us, length us, event | category | flops | bytes accessed | tf_op | source)
XLA Modules:
  0.0 19.5 jit_solution(3040862201594951566)
XLA Ops:
  0.0 18.9 %shard_map.64 = bf16[4,512]{1,0:T(4,128)(2,1)S(1)} custom-call(s32[1,4]{1,0:T(1,128)} %lens_hbm.1, bf16[256,14336]{1,0:T(8,128)(2,1)} %acts_hbm.1, bf16[256,4096]{1,0:T(8,128)(2,1)} %grads_hbm.1, bf16[64,14336]{1,0:T(8,128)(2,1)} %bitcast.2, bf16[64,4096]{1,0:T(8,128)(2,1)} %bitcast.3, bf16[32,4096]{1,0:T(8,128)(2,1)} %q_hbm.1), custom_call_target="tpu_custom_call" | custom-call | tf_op jit(solution)/shard_map/pallas_call | solution.py:232
  18.9 0.6 %copy.8 = bf16[4,512]{1,0:T(4,128)(2,1)} copy(bf16[4,512]{1,0:T(4,128)(2,1)S(1)} %shard_map.64) | data formatting | bytes 8192

commit v2 on v1

--- a/solution.py
+++ b/solution.py
@@ -10,7 +10,8 @@
 MESH = pl.DeviceIdType.MESH
 NT = (((1,), (1,)), ((), ()))
 NN = (((1,), (0,)), ((), ()))
-PIECES = 8
+SHARES = (4, 4, 4, 4, 4, 4, 2, 2)
+PIECES = len(SHARES)
 EARLY = 1
 AHEAD = 4
 GROUP = 4
@@ -35,6 +36,7 @@
     qs,
     eg,
     stage,
+    wide,
     local_sem,
     piece_sem,
     send_sem,
@@ -56,21 +58,20 @@
     tiles = span // LANES
     half = tiles * ROWS
     cols = GROUP * nq
-    piece = ff // PIECES
+    bounds = [ff * sum(SHARES[:p]) // sum(SHARES) for p in range(PIECES + 1)]
 
     backward = (group < n_groups - group).astype(jnp.int32)
 
-    def project(rows, weights, at, size):
-        parts = []
+    def project(sums, rows, weights, first, last):
         for h in range(2):
-            first = at + h * (size // 2 // LANES * LANES)
-            last = at + (size // 2 // LANES * LANES if h == 0 else size)
-            one = weights[:, first:last]
-            twice = jnp.concatenate([one, one], axis=0)
-            parts.append(
-                lax.dot_general(rows[:, first:last], twice, NT, preferred_element_type=jnp.float32)
+            side = slice(h * tokens // 2, (h + 1) * tokens // 2)
+            part = lax.dot_general(
+                weights[:, first:last],
+                rows[side, first:last],
+                NT,
+                preferred_element_type=jnp.float32,
             )
-        return parts[0] + parts[1]
+            sums[h] = part if sums[h] is None else sums[h] + part
 
     def turn(t):
         return t + backward * (n_groups - 2 * t)
@@ -91,7 +92,7 @@
     load_lens = start(lens_hbm, lens, local_sem.at[1])
     load_wout = start(wout_hbm, wout, local_sem.at[2])
     load_grads = start(grads_hbm, grads, local_sem.at[2])
-    pieces = [pl.ds(p * piece, piece) for p in range(PIECES)]
+    pieces = [pl.ds(bounds[p], bounds[p + 1] - bounds[p]) for p in range(PIECES)]
     loads = {}
 
     def fetch(p):
@@ -143,30 +144,39 @@
         mask = jnp.where((row_ex == e) & (token >= first) & (token < end), 1.0, mask)
         first = end
 
-    r_id = lax.broadcasted_iota(jnp.int32, (2 * half, 2 * rank), 0)
-    c_id = lax.broadcasted_iota(jnp.int32, (2 * half, 2 * rank), 1)
-    odd = (r_id >= half).astype(jnp.int32)
-    inner = r_id - odd * half
-    source = 2 * (lax.rem(inner // ex, slots) * tiles + inner // ROWS) + odd
+    r_id = lax.broadcasted_iota(jnp.int32, (2 * half, rank), 0)
+    c_id = lax.broadcasted_iota(jnp.int32, (2 * half, rank), 1)
+    second = (r_id >= half).astype(jnp.int32)
+    inner = r_id - second * half
+    source = 2 * (lax.rem(inner // ex, slots) * tiles + inner // ROWS) + second
     expand = jnp.where(source == c_id, 1.0, 0.0).astype(jnp.bfloat16)
 
     load_wout.wait()
     load_grads.wait()
-    proj_grads = project(grads, wout, 0, wout.shape[1]).astype(jnp.bfloat16)
-    wide = lax.dot_general(expand, proj_grads, NT, preferred_element_type=jnp.float32)
-    wide = wide.reshape(2 * half // 8, 8, tokens) * mask[None]
-    wide = wide.reshape(2 * half, tokens).astype(jnp.bfloat16)
-
-    total = jnp.zeros((tokens, 2 * rank), jnp.float32)
+    sums = [None, None]
+    project(sums, grads, wout, 0, wout.shape[1])
+    proj_grads = jnp.concatenate(sums, axis=1).astype(jnp.bfloat16)
+
+    sums = [None, None]
     for p in range(PIECES):
         for load in loads[p]:
             load.wait()
         fetch(p + AHEAD)
-        total = total + project(acts, win, p * piece, piece)
-    proj_acts = total.astype(jnp.bfloat16)
-    outer = lax.dot_general(wide, proj_acts, NN, preferred_element_type=jnp.float32)
+        project(sums, acts, win, bounds[p], bounds[p + 1])
+        if p == 0:
+            for h in range(2):
+                side = slice(h * half, (h + 1) * half)
+                part = lax.dot_general(
+                    expand[side], proj_grads, NN, preferred_element_type=jnp.float32
+                )
+                part = part.reshape(half // 8, 8, tokens) * mask[None]
+                wide[side] = part.reshape(half, tokens).astype(jnp.bfloat16)
+    proj_acts = jnp.concatenate(sums, axis=1).astype(jnp.bfloat16)
+    twice = jnp.concatenate([proj_acts, proj_acts], axis=0)
+    even = lax.dot_general(wide[:half], twice, NT, preferred_element_type=jnp.float32)
+    odd = lax.dot_general(wide[half:], twice, NT, preferred_element_type=jnp.float32)
     lower = lax.broadcasted_iota(jnp.int32, (half, 2 * rank), 1) < rank
-    eg[group] = jnp.where(lower, outer[:half], outer[half:]).astype(jnp.bfloat16)
+    eg[group] = jnp.where(lower, even, odd).astype(jnp.bfloat16)
 
     eg_copies = []
     for t in range(1, n_groups):
@@ -188,19 +198,17 @@
             jnp.concatenate([one[ROWS * t : ROWS * (t + 1)] for t in range(tiles)], axis=1)
         )
     stacked = jnp.concatenate(stacked, axis=0)
-    scores = [jnp.zeros((ex, cols), jnp.float32) for _ in range(n_groups)]
-    for s in range(slots):
-        relays[s].wait_recv()
-        queries = qs[:, :, pl.ds(s * span, span)].reshape(cols, span)
-        term = 0.0
-        for h in range(2):
-            side = slice(h * (span // 2), (h + 1) * (span // 2))
-            term = term + lax.dot_general(
-                stacked[:, side], queries[:, side], NT, preferred_element_type=jnp.float32
-            )
-        for g in range(n_groups):
-            row = ROWS * g + ex * s
-            scores[g] = scores[g] + term[row : row + ex]
+    scores = [None] * n_groups
+    for early in (range(slots - 1), range(slots - 1, slots)):
+        for s in early:
+            relays[s].wait_recv()
+        for s in early:
+            queries = qs[:, :, pl.ds(s * span, span)].reshape(cols, span)
+            term = lax.dot_general(stacked, queries, NT, preferred_element_type=jnp.float32)
+            for g in range(n_groups):
+                row = ROWS * g + ex * s
+                part = term[row : row + ex]
+                scores[g] = part if scores[g] is None else scores[g] + part
     for g in range(n_groups):
         stage[g] = scores[g].astype(jnp.bfloat16)
 
@@ -243,6 +251,7 @@
             pltpu.VMEM((GROUP, nq, params), bf16),
             pltpu.VMEM((n_groups, ex * params // LANES, LANES), bf16),
             pltpu.VMEM((n_groups, ex, GROUP * nq), bf16),
+            pltpu.VMEM((2 * ex * params // LANES, tokens), bf16),
             dma((3,)),
             dma((PIECES,)),
             dma,

time: 19.7 us -> 18 us (0.914)
  Pallas kernels: 18.9 us -> 17.3 us
    pallas_call x1, Pallas kernels: 18.9 us -> 17.3 us  [local(): pl.pallas_call(functools.partial(kernel, n), out_shape=jax.ShapeDtypeStru...]
where the time goes in v2:
time: 18 us; the launch traced here: 17.9 us
  Pallas kernels  17.3 us (96%)
  local copies, waits for them, and re-layouts  0.6 us (3%)
    pallas_call x1, Pallas kernels, local(): pl.pallas_call(functools.partial(kernel, n), out_shape=jax.ShapeDtypeStru...  17.3 us
    unnamed x1, local copies, waits for them, and re-layouts  0.6 us

profile of v2, /device:TPU:0, one launch (start us, length us, event | category | flops | bytes accessed | tf_op | source)
XLA Modules:
  0.0 17.9 jit_solution(11401200762127743431)
XLA Ops:
  0.0 17.3 %shard_map.64 = bf16[4,512]{1,0:T(4,128)(2,1)S(1)} custom-call(s32[1,4]{1,0:T(1,128)} %lens_hbm.1, bf16[256,14336]{1,0:T(8,128)(2,1)} %acts_hbm.1, bf16[256,4096]{1,0:T(8,128)(2,1)} %grads_hbm.1, bf16[64,14336]{1,0:T(8,128)(2,1)} %bitcast.2, bf16[64,4096]{1,0:T(8,128)(2,1)} %bitcast.3, bf16[32,4096]{1,0:T(8,128)(2,1)} %q_hbm.1), custom_call_target="tpu_custom_call" | custom-call | tf_op jit(solution)/shard_map/pallas_call | solution.py:240
  17.3 0.6 %copy.8 = bf16[4,512]{1,0:T(4,128)(2,1)} copy(bf16[4,512]{1,0:T(4,128)(2,1)S(1)} %shard_map.64) | data formatting | bytes 8192

commit v3 on v1

v3 whole, which is shorter than its diff:
```python
import functools

import jax
import jax.numpy as jnp
from jax import lax
from jax.experimental import pallas as pl
from jax.experimental.pallas import tpu as pltpu
from jax.sharding import PartitionSpec as P

MESH = pl.DeviceIdType.MESH
NT = (((1,), (1,)), ((), ()))
NN = (((1,), (0,)), ((), ()))
GRAD_SHARES = (1,)
SHARES = (4, 4, 4, 4, 4, 4, 2, 1, 1)
EARLY = 0
AHEAD = 5
GROUP = 4
CORES = 2
LANES = 128
ROWS = 16


def kernel(
    n,
    lens_hbm,
    acts_hbm,
    grads_hbm,
    win_hbm,
    wout_hbm,
    q_hbm,
    out,
    lens,
    acts,
    grads,
    win,
    wout,
    q_own,
    qs,
    g_own,
    eg,
    stage,
    res,
    wide,
    gt,
    q_sem,
    grads_sem,
    acts_sem,
    send_sem,
    buddy_recv,
    across_recv,
    eg_recv,
    res_recv,
):
    me = lax.axis_index("dp")
    n_groups = n // GROUP
    group, lane = me // GROUP, lax.rem(me, GROUP)
    core = lax.rem(me, CORES)
    pair = lane - core
    far_pair = CORES - pair
    tokens, ff = acts.shape
    rank, d = wout.shape
    ex = stage.shape[1]
    slots = ROWS // ex
    nq, part = qs.shape[1:]
    span = part // slots
    tiles = span // LANES
    half = tiles * ROWS
    cols = GROUP * nq
    units = CORES * n_groups

    backward = (group < n_groups - group).astype(jnp.int32)

    def peer_group(t):
        return lax.rem(group + t + backward * (n_groups - 2 * t), n_groups)

    def device(g, c):
        return g * GROUP + pair + c

    buddy = device(group, 1 - core)
    across = [group * GROUP + far_pair + c for c in range(CORES)]

    def start(source, target, sem):
        load = pltpu.make_async_copy(source, target, sem)
        load.start()
        return load

    def cuts(size, shares):
        edges = [size * sum(shares[:p]) // sum(shares) for p in range(len(shares) + 1)]
        return list(zip(edges[:-1], edges[1:]))

    def fetch(rows_hbm, rows, weights_hbm, weights, sem, cut):
        side = pl.ds(cut[0], cut[1] - cut[0])
        return (
            start(weights_hbm.at[:, side], weights.at[:, side], sem),
            start(rows_hbm.at[:, side], rows.at[:, side], sem),
        )

    def project(sums, rows, weights, cut):
        for h in range(2):
            side = slice(h * tokens // 2, (h + 1) * tokens // 2)
            term = lax.dot_general(
                rows[side, cut[0] : cut[1]],
                weights[:, cut[0] : cut[1]],
                NT,
                preferred_element_type=jnp.float32,
            )
            sums[h] = term if sums[h] is None else sums[h] + term

    def send(source, target, recv_sem, other):
        copy = pltpu.make_async_remote_copy(
            src_ref=source,
            dst_ref=target,
            send_sem=send_sem,
            recv_sem=recv_sem,
            device_id={"dp": other},
            device_id_type=MESH,
        )
        copy.start()
        return copy

    mine = pl.ds(pl.multiple_of(core * part, LANES), part)
    load_q = start(q_hbm, q_own, q_sem)
    load_lens = start(lens_hbm, lens, grads_sem.at[0])
    grad_cuts, cut = cuts(d, GRAD_SHARES), cuts(ff, SHARES)
    load_grads = [
        fetch(grads_hbm, grads, wout_hbm, wout, grads_sem.at[p], grad_cuts[p])
        for p in range(len(grad_cuts))
    ]
    load_acts = {}

    def fetch_acts(p):
        if p < len(cut):
            load_acts[p] = fetch(acts_hbm, acts, win_hbm, win, acts_sem.at[p], cut[p])

    for p in range(EARLY):
        fetch_acts(p)

    barrier = pltpu.get_barrier_semaphore()
    column = [device(peer_group(t), c) for t in range(1, n_groups) for c in range(CORES)]
    partners = column + [buddy] + across
    for other in partners:
        pl.semaphore_signal(barrier, inc=1, device_id={"dp": other}, device_id_type=MESH)

    load_q.wait()
    for p in range(EARLY, AHEAD):
        fetch_acts(p)
    load_mine = start(q_hbm.at[:, mine], qs.at[lane], q_sem)
    pl.semaphore_wait(barrier, len(partners))
    copies = []
    for c in range(CORES):
        side = pl.ds(c * part, part)
        copies.append(send(q_own.at[:, side], qs.at[lane], across_recv, across[c]))
    other_half = pl.ds(pl.multiple_of((1 - core) * part, LANES), part)
    copies.append(send(q_own.at[:, other_half], qs.at[lane], buddy_recv, buddy))

    load_lens.wait()
    for load in load_grads[0]:
        load.wait()
    sums = [None, None]
    for p in range(len(grad_cuts)):
        if p > 0:
            for load in load_grads[p]:
                load.wait()
        project(sums, grads, wout, grad_cuts[p])
    token = lax.broadcasted_iota(jnp.int32, (8, tokens), 1)
    row_ex = lax.rem(lax.broadcasted_iota(jnp.int32, (8, tokens), 0), ex)
    first = jnp.int32(0)
    mask = jnp.zeros((8, tokens), jnp.float32)
    for e in range(ex):
        end = first + lens[0, e]
        mask = jnp.where((row_ex == e) & (token >= first) & (token < end), 1.0, mask)
        first = end
    gt[...] = jnp.concatenate(sums, axis=0).T

    at_row = lax.broadcasted_iota(jnp.int32, (8, tokens), 0)
    per_block = 8 // ex

    def widen(odd):
        for c, t in [(c, t) for c in range(CORES) for t in range(tiles)]:
            blocks = []
            for b in range(ROWS // 8):
                block = None
                for j in range(per_block):
                    s = b * per_block + j
                    row = 2 * ((c * slots + s) * tiles + t) + odd
                    one = jnp.broadcast_to(gt[row : row + 1], (8, tokens))
                    block = one if block is None else jnp.where(at_row >= j * ex, one, block)
                blocks.append(block * mask)
            at = c * half + t * ROWS
            wide[odd, at : at + ROWS] = jnp.concatenate(blocks, axis=0).astype(jnp.bfloat16)

    sums = [None, None]
    for p in range(len(cut)):
        for load in load_acts[p]:
            load.wait()
        fetch_acts(p + AHEAD)
        project(sums, acts, win, cut[p])
        if p < 2:
            widen(p)
    proj_acts = jnp.concatenate(sums, axis=0).astype(jnp.bfloat16)
    twice = jnp.concatenate([proj_acts, proj_acts], axis=1)
    even = lax.dot_general(wide[0], twice, NN, preferred_element_type=jnp.float32)
    odd = lax.dot_general(wide[1], twice, NN, preferred_element_type=jnp.float32)
    lower = lax.broadcasted_iota(jnp.int32, (CORES * half, 2 * rank), 1) < rank
    both = jnp.where(lower, even, odd).astype(jnp.bfloat16)
    for c in range(CORES):
        g_own[c] = both[c * half : (c + 1) * half]

    unit = group * CORES + core
    for t in range(1, n_groups):
        for c in range(CORES):
            copies.append(send(g_own.at[c], eg.at[unit], eg_recv, device(peer_group(t), c)))
    copies.append(send(g_own.at[1 - core], eg.at[unit], eg_recv, buddy))
    eg[unit] = g_own[core]

    load_mine.wait()
    copies[2].wait_recv()
    both_lanes = qs.at[pl.ds(far_pair, CORES)]
    pltpu.make_async_copy(both_lanes, both_lanes, across_recv).wait()
    rest = eg.at[pl.ds(0, units - 1)]
    pltpu.make_async_copy(rest, rest, eg_recv).wait()

    stacked = []
    for u in range(units):
        one = eg[u]
        stacked.append(
            jnp.concatenate([one[ROWS * t : ROWS * (t + 1)] for t in range(tiles)], axis=1)
        )
    stacked = jnp.concatenate(stacked, axis=0)
    scores = [None] * units
    for s in range(slots):
        queries = qs[:, :, s * span : (s + 1) * span].reshape(cols, span)
        term = lax.dot_general(stacked, queries, NT, preferred_element_type=jnp.float32)
        for u in range(units):
            row = ROWS * u + ex * s
            piece = term[row : row + ex]
            scores[u] = piece if scores[u] is None else scores[u] + piece
    for u in range(units):
        stage[u] = scores[u]

    slot = core * n_groups + group
    for t in range(1, n_groups):
        g = peer_group(t)
        for c in range(CORES):
            copies.append(send(stage.at[g * CORES + c], res.at[slot], res_recv, device(g, c)))
    copies.append(send(stage.at[group * CORES + 1 - core], res.at[slot], res_recv, buddy))
    res[slot] = stage[unit]
    rest = res.at[pl.ds(0, units - 1)]
    pltpu.make_async_copy(rest, rest, res_recv).wait()
    for g in range(n_groups):
        total = res[g] + res[n_groups + g]
        out[:, g * cols : (g + 1) * cols] = total.astype(jnp.bfloat16)
    for copy in copies:
        copy.wait_send()


def local(n, activations, out_grads, lengths, proj_in, proj_out, queries):
    tokens, ff = activations.shape
    d = out_grads.shape[1]
    rank = proj_in.shape[1]
    ex = lengths.shape[1]
    nq, params = queries.shape
    n_groups = n // GROUP
    units = CORES * n_groups
    rows = ex * params // LANES
    bf16, f32 = jnp.bfloat16, jnp.float32
    dma = pltpu.SemaphoreType.DMA
    hbm = pl.BlockSpec(memory_space=pltpu.MemorySpace.HBM)
    return pl.pallas_call(
        functools.partial(kernel, n),
        out_shape=jax.ShapeDtypeStruct((ex, nq * n), bf16),
        in_specs=[hbm] * 6,
        out_specs=pl.BlockSpec(memory_space=pltpu.MemorySpace.VMEM),
        scratch_shapes=[
            pltpu.SMEM((1, ex), jnp.int32),
            pltpu.VMEM((tokens, ff), bf16),
            pltpu.VMEM((tokens, d), bf16),
            pltpu.VMEM((rank, ff), bf16),
            pltpu.VMEM((rank, d), bf16),
            pltpu.VMEM((nq, params), bf16),
            pltpu.VMEM((GROUP, nq, params // CORES), bf16),
            pltpu.VMEM((CORES, rows // CORES, LANES), bf16),
            pltpu.VMEM((units, rows // CORES, LANES), bf16),
            pltpu.VMEM((units, ex, GROUP * nq), f32),
            pltpu.VMEM((units, ex, GROUP * nq), f32),
            pltpu.VMEM((2, rows, tokens), bf16),
            pltpu.VMEM((rank, tokens), f32),
            dma,
            dma((len(GRAD_SHARES),)),
            dma((len(SHARES),)),
            dma,
            dma,
            dma,
            dma,
            dma,
        ],
        compiler_params=pltpu.CompilerParams(
            collective_id=0, has_side_effects=True, vmem_limit_bytes=56500000
        ),
    )(pltpu.with_memory_space_constraint(lengths, pltpu.HBM), activations, out_grads, proj_in.T, proj_out.T, queries)


def solution(mesh):
    in_specs = (
        P(("parts", "dp"), None),
        P(("parts", "dp"), None),
        P(("parts", "dp"), None),
        P(),
        P(),
        P(("parts", "dp"), None),
    )
    out_specs = P(("parts", "dp"), None)
    body = functools.partial(local, mesh.shape["dp"])
    return jax.shard_map(body, mesh=mesh, in_specs=in_specs, out_specs=out_specs, check_vma=False)
```

time: 19.7 us -> 17 us (0.86)
  Pallas kernels: 18.9 us -> 16.3 us
    pallas_call x1, Pallas kernels: 18.9 us -> 16.3 us  [local(): pl.pallas_call(functools.partial(kernel, n), out_shape=jax.ShapeDtypeStru...]
where the time goes in v3:
time: 17 us; the launch traced here: 16.9 us
  Pallas kernels  16.3 us (96%)
  local copies, waits for them, and re-layouts  0.6 us (4%)
    pallas_call x1, Pallas kernels, local(): pl.pallas_call(functools.partial(kernel, n), out_shape=jax.ShapeDtypeStru...  16.3 us
    unnamed x1, local copies, waits for them, and re-layouts  0.6 us

profile of v3, /device:TPU:0, one launch (start us, length us, event | category | flops | bytes accessed | tf_op | source)
XLA Modules:
  0.0 16.9 jit_solution(15216380029418412120)
XLA Ops:
  0.0 16.3 %shard_map.64 = bf16[4,512]{1,0:T(4,128)(2,1)S(1)} custom-call(s32[1,4]{1,0:T(1,128)} %lens_hbm.1, bf16[256,14336]{1,0:T(8,128)(2,1)} %acts_hbm.1, bf16[256,4096]{1,0:T(8,128)(2,1)} %grads_hbm.1, bf16[64,14336]{1,0:T(8,128)(2,1)} %bitcast.2, bf16[64,4096]{1,0:T(8,128)(2,1)} %bitcast.3, bf16[32,4096]{1,0:T(8,128)(2,1)} %q_hbm.1), custom_call_target="tpu_custom_call" | custom-call | tf_op jit(solution)/shard_map/pallas_call | solution.py:269
  16.3 0.6 %copy.8 = bf16[4,512]{1,0:T(4,128)(2,1)} copy(bf16[4,512]{1,0:T(4,128)(2,1)S(1)} %shard_map.64) | data formatting | bytes 8192

commit v4 on v3

--- a/solution.py
+++ b/solution.py
@@ -10,10 +10,8 @@
 MESH = pl.DeviceIdType.MESH
 NT = (((1,), (1,)), ((), ()))
 NN = (((1,), (0,)), ((), ()))
-GRAD_SHARES = (1,)
+GRAD_SHARES = (1, 1)
 SHARES = (4, 4, 4, 4, 4, 4, 2, 1, 1)
-EARLY = 0
-AHEAD = 5
 GROUP = 4
 CORES = 2
 LANES = 128
@@ -106,8 +104,8 @@
             )
             sums[h] = term if sums[h] is None else sums[h] + term
 
-    def send(source, target, recv_sem, other):
-        copy = pltpu.make_async_remote_copy(
+    def remote(source, target, recv_sem, other):
+        return pltpu.make_async_remote_copy(
             src_ref=source,
             dst_ref=target,
             send_sem=send_sem,
@@ -115,43 +113,52 @@
             device_id={"dp": other},
             device_id_type=MESH,
         )
+
+    def send(source, target, recv_sem, other):
+        copy = remote(source, target, recv_sem, other)
         copy.start()
         return copy
 
     mine = pl.ds(pl.multiple_of(core * part, LANES), part)
-    load_q = start(q_hbm, q_own, q_sem)
-    load_lens = start(lens_hbm, lens, grads_sem.at[0])
-    grad_cuts, cut = cuts(d, GRAD_SHARES), cuts(ff, SHARES)
-    load_grads = [
-        fetch(grads_hbm, grads, wout_hbm, wout, grads_sem.at[p], grad_cuts[p])
-        for p in range(len(grad_cuts))
-    ]
-    load_acts = {}
-
-    def fetch_acts(p):
-        if p < len(cut):
-            load_acts[p] = fetch(acts_hbm, acts, win_hbm, win, acts_sem.at[p], cut[p])
-
-    for p in range(EARLY):
-        fetch_acts(p)
-
     barrier = pltpu.get_barrier_semaphore()
     column = [device(peer_group(t), c) for t in range(1, n_groups) for c in range(CORES)]
-    partners = column + [buddy] + across
-    for other in partners:
-        pl.semaphore_signal(barrier, inc=1, device_id={"dp": other}, device_id_type=MESH)
+    partners = across + [buddy] + column
+    waiting = list(partners)
+
+    def announce(count):
+        for other in waiting[:count]:
+            pl.semaphore_signal(barrier, inc=1, device_id={"dp": other}, device_id_type=MESH)
+        del waiting[:count]
+
+    grad_cuts, cut = cuts(d, GRAD_SHARES), cuts(ff, SHARES)
+    load_q = start(q_hbm, q_own, q_sem)
+    announce(3)
+    load_lens = start(lens_hbm, lens, grads_sem.at[0])
+    load_grads, load_acts = [], []
+    for p in range(len(grad_cuts)):
+        load_grads.append(fetch(grads_hbm, grads, wout_hbm, wout, grads_sem.at[p], grad_cuts[p]))
+        announce(1)
+    for p in range(len(cut)):
+        load_acts.append(fetch(acts_hbm, acts, win_hbm, win, acts_sem.at[p], cut[p]))
+        announce(1)
+    announce(len(waiting))
 
     load_q.wait()
-    for p in range(EARLY, AHEAD):
-        fetch_acts(p)
+    other_half = pl.ds(pl.multiple_of((1 - core) * part, LANES), part)
+    copies = [
+        remote(q_own.at[:, pl.ds(c * part, part)], qs.at[lane], across_recv, across[c])
+        for c in range(CORES)
+    ]
+    copies.append(remote(q_own.at[:, other_half], qs.at[lane], buddy_recv, buddy))
+
+    def meet():
+        pl.semaphore_wait(barrier, len(partners))
+        for copy in copies[:3]:
+            copy.start()
+
+    lower_half = group < n_groups // 2
+    pl.when(jnp.logical_not(lower_half))(meet)
     load_mine = start(q_hbm.at[:, mine], qs.at[lane], q_sem)
-    pl.semaphore_wait(barrier, len(partners))
-    copies = []
-    for c in range(CORES):
-        side = pl.ds(c * part, part)
-        copies.append(send(q_own.at[:, side], qs.at[lane], across_recv, across[c]))
-    other_half = pl.ds(pl.multiple_of((1 - core) * part, LANES), part)
-    copies.append(send(q_own.at[:, other_half], qs.at[lane], buddy_recv, buddy))
 
     load_lens.wait()
     for load in load_grads[0]:
@@ -189,11 +196,11 @@
             at = c * half + t * ROWS
             wide[odd, at : at + ROWS] = jnp.concatenate(blocks, axis=0).astype(jnp.bfloat16)
 
+    pl.when(lower_half)(meet)
     sums = [None, None]
     for p in range(len(cut)):
         for load in load_acts[p]:
             load.wait()
-        fetch_acts(p + AHEAD)
         project(sums, acts, win, cut[p])
         if p < 2:
             widen(p)

time: 17 us -> 16.3 us (0.959)
  Pallas kernels: 16.3 us -> 15.6 us
    pallas_call x1, Pallas kernels: 16.3 us -> 15.6 us  [local(): pl.pallas_call(functools.partial(kernel, n), out_shape=jax.ShapeDtypeStru...]
where the time goes in v4:
time: 16.3 us; the launch traced here: 16.2 us
  Pallas kernels  15.6 us (96%)
  local copies, waits for them, and re-layouts  0.6 us (4%)
    pallas_call x1, Pallas kernels, local(): pl.pallas_call(functools.partial(kernel, n), out_shape=jax.ShapeDtypeStru...  15.6 us
    unnamed x1, local copies, waits for them, and re-layouts  0.6 us

profile of v4, /device:TPU:0, one launch (start us, length us, event | category | flops | bytes accessed | tf_op | source)
XLA Modules:
  0.0 16.2 jit_solution(6784644917575130537)
XLA Ops:
  0.0 15.6 %shard_map.64 = bf16[4,512]{1,0:T(4,128)(2,1)S(1)} custom-call(s32[1,4]{1,0:T(1,128)} %lens_hbm.1, bf16[256,14336]{1,0:T(8,128)(2,1)} %acts_hbm.1, bf16[256,4096]{1,0:T(8,128)(2,1)} %grads_hbm.1, bf16[64,14336]{1,0:T(8,128)(2,1)} %bitcast.2, bf16[64,4096]{1,0:T(8,128)(2,1)} %bitcast.3, bf16[32,4096]{1,0:T(8,128)(2,1)} %q_hbm.1), custom_call_target="tpu_custom_call" | custom-call | tf_op jit(solution)/shard_map/pallas_call | solution.py:276
  15.6 0.6 %copy.8 = bf16[4,512]{1,0:T(4,128)(2,1)} copy(bf16[4,512]{1,0:T(4,128)(2,1)S(1)} %shard_map.64) | data formatting | bytes 8192

commit v5 on v4

--- a/solution.py
+++ b/solution.py
@@ -11,7 +11,7 @@
 NT = (((1,), (1,)), ((), ()))
 NN = (((1,), (0,)), ((), ()))
 GRAD_SHARES = (1, 1)
-SHARES = (4, 4, 4, 4, 4, 4, 2, 1, 1)
+SHARES = (4, 6, 6, 6, 4, 2)
 GROUP = 4
 CORES = 2
 LANES = 128
@@ -44,8 +44,7 @@
     grads_sem,
     acts_sem,
     send_sem,
-    buddy_recv,
-    across_recv,
+    q_recv,
     eg_recv,
     res_recv,
 ):
@@ -146,10 +145,10 @@
     load_q.wait()
     other_half = pl.ds(pl.multiple_of((1 - core) * part, LANES), part)
     copies = [
-        remote(q_own.at[:, pl.ds(c * part, part)], qs.at[lane], across_recv, across[c])
+        remote(q_own.at[:, pl.ds(c * part, part)], qs.at[lane], q_recv, across[c])
         for c in range(CORES)
     ]
-    copies.append(remote(q_own.at[:, other_half], qs.at[lane], buddy_recv, buddy))
+    copies.append(remote(q_own.at[:, other_half], qs.at[lane], q_recv, buddy))
 
     def meet():
         pl.semaphore_wait(barrier, len(partners))
@@ -157,32 +156,23 @@
             copy.start()
 
     lower_half = group < n_groups // 2
-    pl.when(jnp.logical_not(lower_half))(meet)
     load_mine = start(q_hbm.at[:, mine], qs.at[lane], q_sem)
-
-    load_lens.wait()
-    for load in load_grads[0]:
-        load.wait()
-    sums = [None, None]
-    for p in range(len(grad_cuts)):
-        if p > 0:
-            for load in load_grads[p]:
-                load.wait()
-        project(sums, grads, wout, grad_cuts[p])
-    token = lax.broadcasted_iota(jnp.int32, (8, tokens), 1)
-    row_ex = lax.rem(lax.broadcasted_iota(jnp.int32, (8, tokens), 0), ex)
-    first = jnp.int32(0)
-    mask = jnp.zeros((8, tokens), jnp.float32)
-    for e in range(ex):
-        end = first + lens[0, e]
-        mask = jnp.where((row_ex == e) & (token >= first) & (token < end), 1.0, mask)
-        first = end
-    gt[...] = jnp.concatenate(sums, axis=0).T
 
     at_row = lax.broadcasted_iota(jnp.int32, (8, tokens), 0)
     per_block = 8 // ex
 
-    def widen(odd):
+    def masks():
+        token = lax.broadcasted_iota(jnp.int32, (8, tokens), 1)
+        row_ex = lax.rem(at_row, ex)
+        begin = jnp.int32(0)
+        mask = jnp.zeros((8, tokens), jnp.float32)
+        for e in range(ex):
+            end = begin + lens[0, e]
+            mask = jnp.where((row_ex == e) & (token >= begin) & (token < end), 1.0, mask)
+            begin = end
+        return mask
+
+    def widen(odd, mask):
         for c, t in [(c, t) for c in range(CORES) for t in range(tiles)]:
             blocks = []
             for b in range(ROWS // 8):
@@ -196,34 +186,56 @@
             at = c * half + t * ROWS
             wide[odd, at : at + ROWS] = jnp.concatenate(blocks, axis=0).astype(jnp.bfloat16)
 
-    pl.when(lower_half)(meet)
-    sums = [None, None]
-    for p in range(len(cut)):
-        for load in load_acts[p]:
-            load.wait()
-        project(sums, acts, win, cut[p])
-        if p < 2:
-            widen(p)
-    proj_acts = jnp.concatenate(sums, axis=0).astype(jnp.bfloat16)
-    twice = jnp.concatenate([proj_acts, proj_acts], axis=1)
-    even = lax.dot_general(wide[0], twice, NN, preferred_element_type=jnp.float32)
-    odd = lax.dot_general(wide[1], twice, NN, preferred_element_type=jnp.float32)
-    lower = lax.broadcasted_iota(jnp.int32, (CORES * half, 2 * rank), 1) < rank
-    both = jnp.where(lower, even, odd).astype(jnp.bfloat16)
+    def produce(meet_late):
+        if not meet_late:
+            meet()
+        load_lens.wait()
+        of_grads = [None, None]
+        for p in range(len(grad_cuts)):
+            for load in load_grads[p]:
+                load.wait()
+            project(of_grads, grads, wout, grad_cuts[p])
+
+        def keep():
+            gt[...] = jnp.concatenate(of_grads, axis=0).T
+
+        if meet_late:
+            keep()
+            meet()
+        of_acts = [None, None]
+        for p in range(len(cut)):
+            for load in load_acts[p]:
+                load.wait()
+            project(of_acts, acts, win, cut[p])
+            if p == 0 and not meet_late:
+                keep()
+            if p == 1:
+                mask = masks()
+                widen(0, mask)
+            if p == 2:
+                widen(1, mask)
+        proj_acts = jnp.concatenate(of_acts, axis=0).astype(jnp.bfloat16)
+        twice = jnp.concatenate([proj_acts, proj_acts], axis=1)
+        even = lax.dot_general(wide[0], twice, NN, preferred_element_type=jnp.float32)
+        odd = lax.dot_general(wide[1], twice, NN, preferred_element_type=jnp.float32)
+        lower = lax.broadcasted_iota(jnp.int32, (CORES * half, 2 * rank), 1) < rank
+        both = jnp.where(lower, even, odd).astype(jnp.bfloat16)
+        for c in range(CORES):
+            g_own[c] = both[c * half : (c + 1) * half]
+
+    pl.when(lower_half)(lambda: produce(True))
+    pl.when(jnp.logical_not(lower_half))(lambda: produce(False))
+
+    unit = group * CORES + core
     for c in range(CORES):
-        g_own[c] = both[c * half : (c + 1) * half]
-
-    unit = group * CORES + core
-    for t in range(1, n_groups):
-        for c in range(CORES):
+        for t in range(1, n_groups):
             copies.append(send(g_own.at[c], eg.at[unit], eg_recv, device(peer_group(t), c)))
     copies.append(send(g_own.at[1 - core], eg.at[unit], eg_recv, buddy))
     eg[unit] = g_own[core]
 
     load_mine.wait()
-    copies[2].wait_recv()
-    both_lanes = qs.at[pl.ds(far_pair, CORES)]
-    pltpu.make_async_copy(both_lanes, both_lanes, across_recv).wait()
+    others = qs.at[pl.ds(0, GROUP - 1)]
+    pltpu.make_async_copy(others, others, q_recv).wait()
     rest = eg.at[pl.ds(0, units - 1)]
     pltpu.make_async_copy(rest, rest, eg_recv).wait()
 
@@ -299,7 +311,6 @@
             dma,
             dma,
             dma,
-            dma,
         ],
         compiler_params=pltpu.CompilerParams(
             collective_id=0, has_side_effects=True, vmem_limit_bytes=56500000

time: 16.3 us -> 16 us (0.982)
  Pallas kernels: 15.6 us -> 15.3 us
    pallas_call x1, Pallas kernels: 15.6 us -> 15.3 us  [local(): pl.pallas_call(functools.partial(kernel, n), out_shape=jax.ShapeDtypeStru...]
where the time goes in v5:
time: 16 us; the launch traced here: 15.9 us
  Pallas kernels  15.3 us (96%)
  local copies, waits for them, and re-layouts  0.6 us (4%)
    pallas_call x1, Pallas kernels, local(): pl.pallas_call(functools.partial(kernel, n), out_shape=jax.ShapeDtypeStru...  15.3 us
    unnamed x1, local copies, waits for them, and re-layouts  0.6 us

profile of v5, /device:TPU:0, one launch (start us, length us, event | category | flops | bytes accessed | tf_op | source)
XLA Modules:
  0.0 15.9 jit_solution(17696191867039681335)
XLA Ops:
  0.0 15.3 %shard_map.64 = bf16[4,512]{1,0:T(4,128)(2,1)S(1)} custom-call(s32[1,4]{1,0:T(1,128)} %lens_hbm.1, bf16[256,14336]{1,0:T(8,128)(2,1)} %acts_hbm.1, bf16[256,4096]{1,0:T(8,128)(2,1)} %grads_hbm.1, bf16[64,14336]{1,0:T(8,128)(2,1)} %bitcast.2, bf16[64,4096]{1,0:T(8,128)(2,1)} %bitcast.3, bf16[32,4096]{1,0:T(8,128)(2,1)} %q_hbm.1), custom_call_target="tpu_custom_call" | custom-call | tf_op jit(solution)/shard_map/pallas_call | solution.py:288
  15.3 0.6 %copy.8 = bf16[4,512]{1,0:T(4,128)(2,1)} copy(bf16[4,512]{1,0:T(4,128)(2,1)S(1)} %shard_map.64) | data formatting | bytes 8192

commit v6 on v5

--- a/solution.py
+++ b/solution.py
@@ -26,7 +26,7 @@
     win_hbm,
     wout_hbm,
     q_hbm,
-    out,
+    res,
     lens,
     acts,
     grads,
@@ -37,7 +37,6 @@
     g_own,
     eg,
     stage,
-    res,
     wide,
     gt,
     q_sem,
@@ -201,7 +200,7 @@
 
         if meet_late:
             keep()
-            meet()
+            pl.when(me >= CORES)(meet)
         of_acts = [None, None]
         for p in range(len(cut)):
             for load in load_acts[p]:
@@ -226,51 +225,88 @@
     pl.when(lower_half)(lambda: produce(True))
     pl.when(jnp.logical_not(lower_half))(lambda: produce(False))
 
+    pl.when(me < CORES)(meet)
     unit = group * CORES + core
+    home = group == 0
+    away = jnp.logical_not(home)
+    kind = jnp.where(home, 0, 1)
     for c in range(CORES):
         for t in range(1, n_groups):
-            copies.append(send(g_own.at[c], eg.at[unit], eg_recv, device(peer_group(t), c)))
-    copies.append(send(g_own.at[1 - core], eg.at[unit], eg_recv, buddy))
+            copies.append(send(g_own.at[c], eg.at[unit], eg_recv.at[kind], device(peer_group(t), c)))
+    copies.append(send(g_own.at[1 - core], eg.at[unit], eg_recv.at[kind], buddy))
     eg[unit] = g_own[core]
 
     load_mine.wait()
     others = qs.at[pl.ds(0, GROUP - 1)]
     pltpu.make_async_copy(others, others, q_recv).wait()
-    rest = eg.at[pl.ds(0, units - 1)]
-    pltpu.make_async_copy(rest, rest, eg_recv).wait()
-
-    stacked = []
-    for u in range(units):
-        one = eg[u]
-        stacked.append(
-            jnp.concatenate([one[ROWS * t : ROWS * (t + 1)] for t in range(tiles)], axis=1)
-        )
-    stacked = jnp.concatenate(stacked, axis=0)
-    scores = [None] * units
-    for s in range(slots):
-        queries = qs[:, :, s * span : (s + 1) * span].reshape(cols, span)
-        term = lax.dot_general(stacked, queries, NT, preferred_element_type=jnp.float32)
-        for u in range(units):
-            row = ROWS * u + ex * s
-            piece = term[row : row + ex]
-            scores[u] = piece if scores[u] is None else scores[u] + piece
-    for u in range(units):
-        stage[u] = scores[u]
-
     slot = core * n_groups + group
+
+    def arrived(count, sem):
+        block = eg.at[pl.ds(0, count)]
+        pltpu.make_async_copy(block, block, sem).wait()
+
+    def score(low, high):
+        stacked = []
+        for u in range(low, high):
+            one = eg[u]
+            stacked.append(
+                jnp.concatenate([one[ROWS * t : ROWS * (t + 1)] for t in range(tiles)], axis=1)
+            )
+        stacked = jnp.concatenate(stacked, axis=0)
+        scores = [None] * (high - low)
+        for s in range(slots):
+            queries = qs[:, :, s * span : (s + 1) * span].reshape(cols, span)
+            term = lax.dot_general(stacked, queries, NT, preferred_element_type=jnp.float32)
+            for u in range(high - low):
+                row = ROWS * u + ex * s
+                piece = term[row : row + ex]
+                scores[u] = piece if scores[u] is None else scores[u] + piece
+        for u in range(low, high):
+            stage[u] = scores[u - low]
+
+    def deliver(u, other):
+        return remote(stage.at[u], res.at[slot], res_recv, other)
+
+    to_buddy = deliver(group * CORES + 1 - core, buddy)
+    to_home = [deliver(c, device(0, c)) for c in range(CORES)]
+    onward = []
     for t in range(1, n_groups):
         g = peer_group(t)
         for c in range(CORES):
-            copies.append(send(stage.at[g * CORES + c], res.at[slot], res_recv, device(g, c)))
-    copies.append(send(stage.at[group * CORES + 1 - core], res.at[slot], res_recv, buddy))
-    res[slot] = stage[unit]
+            onward.append((g > 0, deliver(g * CORES + c, device(g, c))))
+
+    def settle():
+        to_buddy.start()
+        res[slot] = stage[unit]
+
+    pl.when(home)(lambda: arrived(1, eg_recv.at[0]))
+    pl.when(away)(lambda: arrived(CORES, eg_recv.at[0]))
+    score(0, CORES)
+    pl.when(home)(settle)
+
+    @pl.when(away)
+    def _():
+        for copy in to_home:
+            copy.start()
+
+    pl.when(home)(lambda: arrived(units - CORES, eg_recv.at[1]))
+    pl.when(away)(lambda: arrived(units - CORES - 1, eg_recv.at[1]))
+    score(CORES, units)
+    for wanted, copy in onward:
+        pl.when(wanted)(copy.start)
+    pl.when(away)(settle)
     rest = res.at[pl.ds(0, units - 1)]
     pltpu.make_async_copy(rest, rest, res_recv).wait()
-    for g in range(n_groups):
-        total = res[g] + res[n_groups + g]
-        out[:, g * cols : (g + 1) * cols] = total.astype(jnp.bfloat16)
-    for copy in copies:
+    for copy in copies + [to_buddy]:
         copy.wait_send()
+
+    @pl.when(away)
+    def _():
+        for copy in to_home:
+            copy.wait_send()
+
+    for wanted, copy in onward:
+        pl.when(wanted)(copy.wait_send)
 
 
 def local(n, activations, out_grads, lengths, proj_in, proj_out, queries):
@@ -285,9 +321,9 @@
     bf16, f32 = jnp.bfloat16, jnp.float32
     dma = pltpu.SemaphoreType.DMA
     hbm = pl.BlockSpec(memory_space=pltpu.MemorySpace.HBM)
-    return pl.pallas_call(
+    parts = pl.pallas_call(
         functools.partial(kernel, n),
-        out_shape=jax.ShapeDtypeStruct((ex, nq * n), bf16),
+        out_shape=jax.ShapeDtypeStruct((units, ex, GROUP * nq), f32),
         in_specs=[hbm] * 6,
         out_specs=pl.BlockSpec(memory_space=pltpu.MemorySpace.VMEM),
         scratch_shapes=[
@@ -301,7 +337,6 @@
             pltpu.VMEM((CORES, rows // CORES, LANES), bf16),
             pltpu.VMEM((units, rows // CORES, LANES), bf16),
             pltpu.VMEM((units, ex, GROUP * nq), f32),
-            pltpu.VMEM((units, ex, GROUP * nq), f32),
             pltpu.VMEM((2, rows, tokens), bf16),
             pltpu.VMEM((rank, tokens), f32),
             dma,
@@ -309,13 +344,15 @@
             dma((len(SHARES),)),
             dma,
             dma,
-            dma,
+            dma((2,)),
             dma,
         ],
         compiler_params=pltpu.CompilerParams(
             collective_id=0, has_side_effects=True, vmem_limit_bytes=56500000
         ),
     )(pltpu.with_memory_space_constraint(lengths, pltpu.HBM), activations, out_grads, proj_in.T, proj_out.T, queries)
+    total = parts[:n_groups] + parts[n_groups:]
+    return total.swapaxes(0, 1).reshape(ex, nq * n).astype(bf16)
 
 
 def solution(mesh):

time: 16 us -> 15.7 us (0.981)
  other arithmetic: 0 us -> 0.6 us
  local copies, waits for them, and re-layouts: 0.6 us -> 0 us
  Pallas kernels: 15.3 us -> 14.9 us
    convert_element_type x0 -> x1, other arithmetic: none -> 0.6 us  [local(): return total.swapaxes(0, 1).reshape(ex, nq * n).astype(bf16)]
    unnamed x1 -> x0, local copies, waits for them, and re-layouts: 0.6 us -> none
    pallas_call x1, Pallas kernels: 15.3 us -> 14.9 us  [local(): pl.pallas_call(functools.partial(kernel, n), out_shape=jax.ShapeDtypeStru...]
where the time goes in v6:
time: 15.7 us; the launch traced here: 15.6 us
  Pallas kernels  14.9 us (95%)
  other arithmetic  0.6 us (4%)
    pallas_call x1, Pallas kernels, local(): pl.pallas_call(functools.partial(kernel, n), out_shape=jax.ShapeDtypeStru...  14.9 us
    convert_element_type x1, other arithmetic, local(): return total.swapaxes(0, 1).reshape(ex, nq * n).astype(bf16)  0.6 us

profile of v6, /device:TPU:0, one launch (start us, length us, event | category | flops | bytes accessed | tf_op | source)
XLA Modules:
  0.0 15.6 jit_solution(15755893453488321214)
XLA Ops:
  0.0 14.9 %shard_map.64 = f32[8,4,128]{2,1,0:T(4,128)S(1)} custom-call(s32[1,4]{1,0:T(1,128)} %lens_hbm.1, bf16[256,14336]{1,0:T(8,128)(2,1)} %acts_hbm.1, bf16[256,4096]{1,0:T(8,128)(2,1)} %grads_hbm.1, bf16[64,14336]{1,0:T(8,128)(2,1)} %bitcast.6, bf16[64,4096]{1,0:T(8,128)(2,1)} %bitcast.7, bf16[32,4096]{1,0:T(8,128)(2,1)} %q_hbm.1), custom_call_target="tpu_custom_call" | custom-call | tf_op jit(solution)/shard_map/pallas_call | solution.py:324
  15.0 0.6 %fusion = bf16[4,512]{1,0:T(4,128)(2,1)} fusion(f32[8,4,128]{2,1,0:T(4,128)S(1)} %shard_map.64), kind=kLoop, calls=%fused_computation.1 | loop fusion | flops 4096 | bytes 20480 | tf_op jit(solution)/shard_map/convert_element_type | solution.py:355

commit v7 on v6

--- a/solution.py
+++ b/solution.py
@@ -13,6 +13,7 @@
 GRAD_SHARES = (1, 1)
 SHARES = (4, 6, 6, 6, 4, 2)
 GROUP = 4
+FOLDS = 2
 CORES = 2
 LANES = 128
 ROWS = 16
@@ -142,16 +143,18 @@
     announce(len(waiting))
 
     load_q.wait()
-    other_half = pl.ds(pl.multiple_of((1 - core) * part, LANES), part)
-    copies = [
-        remote(q_own.at[:, pl.ds(c * part, part)], qs.at[lane], q_recv, across[c])
-        for c in range(CORES)
-    ]
-    copies.append(remote(q_own.at[:, other_half], qs.at[lane], q_recv, buddy))
+    fold = part // FOLDS
+    copies = []
+    for c, other in ((0, across[0]), (1, across[1]), (1 - core, buddy)):
+        for f in range(FOLDS):
+            side = pl.ds(pl.multiple_of(c * part + f * fold, LANES), fold)
+            into = qs.at[lane, :, pl.ds(f * fold, fold)]
+            copies.append(remote(q_own.at[:, side], into, q_recv.at[f], other))
+    queries_sent = list(copies)
 
     def meet():
         pl.semaphore_wait(barrier, len(partners))
-        for copy in copies[:3]:
+        for copy in queries_sent:
             copy.start()
 
     lower_half = group < n_groups // 2
@@ -237,15 +240,18 @@
     eg[unit] = g_own[core]
 
     load_mine.wait()
-    others = qs.at[pl.ds(0, GROUP - 1)]
-    pltpu.make_async_copy(others, others, q_recv).wait()
+
+    def queries_here(f):
+        others = qs.at[pl.ds(0, GROUP - 1), :, pl.ds(f * fold, fold)]
+        pltpu.make_async_copy(others, others, q_recv.at[f]).wait()
+
     slot = core * n_groups + group
 
     def arrived(count, sem):
         block = eg.at[pl.ds(0, count)]
         pltpu.make_async_copy(block, block, sem).wait()
 
-    def score(low, high):
+    def score(low, high, ready=lambda f: None):
         stacked = []
         for u in range(low, high):
             one = eg[u]
@@ -255,6 +261,8 @@
         stacked = jnp.concatenate(stacked, axis=0)
         scores = [None] * (high - low)
         for s in range(slots):
+            if s % (slots // FOLDS) == 0:
+                ready(s // (slots // FOLDS))
             queries = qs[:, :, s * span : (s + 1) * span].reshape(cols, span)
             term = lax.dot_general(stacked, queries, NT, preferred_element_type=jnp.float32)
             for u in range(high - low):
@@ -281,7 +289,7 @@
 
     pl.when(home)(lambda: arrived(1, eg_recv.at[0]))
     pl.when(away)(lambda: arrived(CORES, eg_recv.at[0]))
-    score(0, CORES)
+    score(0, CORES, queries_here)
     pl.when(home)(settle)
 
     @pl.when(away)
@@ -343,7 +351,7 @@
             dma((len(GRAD_SHARES),)),
             dma((len(SHARES),)),
             dma,
-            dma,
+            dma((FOLDS,)),
             dma((2,)),
             dma,
         ],

time: 15.7 us -> 15.6 us (level)
  no operation moved by 1% of the time
where the time goes in v7:
time: 15.6 us; the launch traced here: 15.5 us
  Pallas kernels  14.9 us (96%)
  other arithmetic  0.6 us (4%)
    pallas_call x1, Pallas kernels, local(): pl.pallas_call(functools.partial(kernel, n), out_shape=jax.ShapeDtypeStru...  14.9 us
    convert_element_type x1, other arithmetic, local(): return total.swapaxes(0, 1).reshape(ex, nq * n).astype(bf16)  0.6 us

profile of v7, /device:TPU:0, one launch (start us, length us, event | category | flops | bytes accessed | tf_op | source)
XLA Modules:
  0.0 15.5 jit_solution(11619218990387952919)
XLA Ops:
  0.0 14.9 %shard_map.64 = f32[8,4,128]{2,1,0:T(4,128)S(1)} custom-call(s32[1,4]{1,0:T(1,128)} %lens_hbm.1, bf16[256,14336]{1,0:T(8,128)(2,1)} %acts_hbm.1, bf16[256,4096]{1,0:T(8,128)(2,1)} %grads_hbm.1, bf16[64,14336]{1,0:T(8,128)(2,1)} %bitcast.6, bf16[64,4096]{1,0:T(8,128)(2,1)} %bitcast.7, bf16[32,4096]{1,0:T(8,128)(2,1)} %q_hbm.1), custom_call_target="tpu_custom_call" | custom-call | tf_op jit(solution)/shard_map/pallas_call | solution.py:332
  14.9 0.6 %fusion = bf16[4,512]{1,0:T(4,128)(2,1)} fusion(f32[8,4,128]{2,1,0:T(4,128)S(1)} %shard_map.64), kind=kLoop, calls=%fused_computation.1 | loop fusion | flops 4096 | bytes 20480 | tf_op jit(solution)/shard_map/convert_element_type | solution.py:363

commit v8 on v7

--- a/solution.py
+++ b/solution.py
@@ -11,7 +11,7 @@
 NT = (((1,), (1,)), ((), ()))
 NN = (((1,), (0,)), ((), ()))
 GRAD_SHARES = (1, 1)
-SHARES = (4, 6, 6, 6, 4, 2)
+SHARES = (4, 8, 8, 6, 2)
 GROUP = 4
 FOLDS = 2
 CORES = 2
@@ -158,7 +158,6 @@
             copy.start()
 
     lower_half = group < n_groups // 2
-    load_mine = start(q_hbm.at[:, mine], qs.at[lane], q_sem)
 
     at_row = lax.broadcasted_iota(jnp.int32, (8, tokens), 0)
     per_block = 8 // ex
@@ -239,7 +238,7 @@
     copies.append(send(g_own.at[1 - core], eg.at[unit], eg_recv.at[kind], buddy))
     eg[unit] = g_own[core]
 
-    load_mine.wait()
+    qs[lane] = q_own[:, mine]
 
     def queries_here(f):
         others = qs.at[pl.ds(0, GROUP - 1), :, pl.ds(f * fold, fold)]

time: 15.6 us -> 15.6 us (level)
  no operation moved by 1% of the time
where the time goes in v8:
time: 15.6 us; the launch traced here: 15.5 us
  Pallas kernels  14.9 us (96%)
  other arithmetic  0.6 us (4%)
    pallas_call x1, Pallas kernels, local(): pl.pallas_call(functools.partial(kernel, n), out_shape=jax.ShapeDtypeStru...  14.9 us
    convert_element_type x1, other arithmetic, local(): return total.swapaxes(0, 1).reshape(ex, nq * n).astype(bf16)  0.6 us

profile of v8, /device:TPU:0, one launch (start us, length us, event | category | flops | bytes accessed | tf_op | source)
XLA Modules:
  0.0 15.5 jit_solution(6903590433260759239)
XLA Ops:
  0.0 14.9 %shard_map.64 = f32[8,4,128]{2,1,0:T(4,128)S(1)} custom-call(s32[1,4]{1,0:T(1,128)} %lens_hbm.1, bf16[256,14336]{1,0:T(8,128)(2,1)} %acts_hbm.1, bf16[256,4096]{1,0:T(8,128)(2,1)} %grads_hbm.1, bf16[64,14336]{1,0:T(8,128)(2,1)} %bitcast.6, bf16[64,4096]{1,0:T(8,128)(2,1)} %bitcast.7, bf16[32,4096]{1,0:T(8,128)(2,1)} %q_hbm.1), custom_call_target="tpu_custom_call" | custom-call | tf_op jit(solution)/shard_map/pallas_call | solution.py:331
  14.9 0.6 %fusion = bf16[4,512]{1,0:T(4,128)(2,1)} fusion(f32[8,4,128]{2,1,0:T(4,128)S(1)} %shard_map.64), kind=kLoop, calls=%fused_computation.1 | loop fusion | flops 4096 | bytes 20480 | tf_op jit(solution)/shard_map/convert_element_type | solution.py:362

commit v9 on v8

--- a/solution.py
+++ b/solution.py
@@ -13,7 +13,7 @@
 GRAD_SHARES = (1, 1)
 SHARES = (4, 8, 8, 6, 2)
 GROUP = 4
-FOLDS = 2
+FOLDS = 4
 CORES = 2
 LANES = 128
 ROWS = 16

time: 15.6 us -> 15.6 us (level)
  no operation moved by 1% of the time
where the time goes in v9:
time: 15.6 us; the launch traced here: 15.5 us
  Pallas kernels  14.9 us (96%)
  other arithmetic  0.6 us (4%)
    pallas_call x1, Pallas kernels, local(): pl.pallas_call(functools.partial(kernel, n), out_shape=jax.ShapeDtypeStru...  14.9 us
    convert_element_type x1, other arithmetic, local(): return total.swapaxes(0, 1).reshape(ex, nq * n).astype(bf16)  0.6 us

profile of v9, /device:TPU:0, one launch (start us, length us, event | category | flops | bytes accessed | tf_op | source)
XLA Modules:
  0.0 15.5 jit_solution(14027316537374743342)
XLA Ops:
  0.0 14.9 %shard_map.64 = f32[8,4,128]{2,1,0:T(4,128)S(1)} custom-call(s32[1,4]{1,0:T(1,128)} %lens_hbm.1, bf16[256,14336]{1,0:T(8,128)(2,1)} %acts_hbm.1, bf16[256,4096]{1,0:T(8,128)(2,1)} %grads_hbm.1, bf16[64,14336]{1,0:T(8,128)(2,1)} %bitcast.6, bf16[64,4096]{1,0:T(8,128)(2,1)} %bitcast.7, bf16[32,4096]{1,0:T(8,128)(2,1)} %q_hbm.1), custom_call_target="tpu_custom_call" | custom-call | tf_op jit(solution)/shard_map/pallas_call | solution.py:331
  14.9 0.6 %fusion = bf16[4,512]{1,0:T(4,128)(2,1)} fusion(f32[8,4,128]{2,1,0:T(4,128)S(1)} %shard_map.64), kind=kLoop, calls=%fused_computation.1 | loop fusion | flops 4096 | bytes 20480 | tf_op jit(solution)/shard_map/convert_element_type | solution.py:362
